TPU v7x, 32 devices: a whole 2x2x4 slice. The times are simulated.
32 devices in a mesh: rows: 16 (over z, y, x), cols: 2 (over core).
Axes of the slice: x: 2, y: 2, z: 4, core: 2. Of those that a mesh axis runs over, the one named last changes fastest.
Arguments:
- green: float32 [2, 4096, 4096], P('cols', 'rows'), may hold values from -1 to 1, as said below
- sites: int32 [16], replicated, may hold values from 0 to 4095, as said below
- fields: int32 [4096], replicated, may hold values from 0 to 1
- accept: int32 [16], replicated, may hold values 0 or 1
Outputs:
- green_new: float32 [2, 4096, 4096], P('cols', 'rows')
- log_weight: float32 [], replicated
Inputs may be any that keep to these rules, and one draw needn't show every extreme that they name: The 16 proposed sites are distinct. `green`: each spin's matrix has its diagonal within 0.1 to 0.9 and off-diagonal entries of size about 1 / sqrt(4096).
All inputs are finite; a program needn't handle non-finite values.
Results may differ from a plain program's by a relative error of at most 0.0003.
Values sent between devices are 32-bit elements; how exact they have to be, the bound alone decides.
A program may use at most 64 MiB of HBM per device.

v0:
```python
import jax
import jax.numpy as jnp
from jax import lax
from jax.sharding import PartitionSpec as P

FLOOR = 0.25
COUPLING = 0.5


def on_device(green, sites, fields, accept):
    local = green[0]
    rows_dev = local.shape[0]
    width = local.shape[1]
    steps = sites.shape[0]
    first = lax.axis_index("rows") * rows_dev
    sigma = 1.0 - 2.0 * lax.axis_index("cols").astype(jnp.float32)
    spins = 1.0 - 2.0 * jnp.take(fields, sites).astype(jnp.float32)
    deltas = jnp.exp(-2.0 * COUPLING * sigma * spins) - 1.0
    flags = accept.astype(jnp.float32)
    positions = lax.broadcasted_iota(jnp.int32, (1, width), 1)

    def advance(k, row, u_loc, v_all, weight):
        site = sites[k]
        v_site = lax.dynamic_slice_in_dim(v_all, site, 1, 0)
        column = lax.dynamic_slice_in_dim(local, site, 1, 1)[:, 0] - jnp.dot(
            u_loc, v_site[0], precision=lax.Precision.HIGHEST
        )
        diag = lax.dynamic_slice_in_dim(row[0], site, 1)[0]
        ratio = jnp.maximum(1.0 + deltas[k] * (1.0 - diag), FLOOR)
        coef = flags[k] * deltas[k] / ratio
        u_loc = lax.dynamic_update_slice_in_dim(u_loc, (coef * column)[:, None], k, 1)
        fresh = (positions == site).astype(jnp.float32) - row
        v_all = lax.dynamic_update_slice_in_dim(v_all, fresh.T, k, 1)
        weight = weight + flags[k] * jnp.log(ratio)
        return (u_loc, v_all, weight, coef, v_site)

    u_start = jnp.zeros((rows_dev, steps), jnp.float32)
    v_start = jnp.zeros((width, steps), jnp.float32)
    w_start = jnp.zeros((), jnp.float32)
    inside = ((sites >= first) & (sites < first + rows_dev)).astype(jnp.float32)
    picked = jnp.take(local, jnp.clip(sites - first, 0, rows_dev - 1), axis=0) * inside[:, None]
    raw_rows = lax.psum(picked, "rows")
    block = jnp.take(raw_rows, sites, axis=1)

    def step(k, state):
        u_loc, v_all, weight, u_sites = state
        row = lax.dynamic_slice_in_dim(raw_rows, k, 1, 0) - jnp.dot(
            lax.dynamic_slice_in_dim(u_sites, k, 1, 0), v_all.T, precision=lax.Precision.HIGHEST
        )
        u_loc, v_all, weight, coef, v_site = advance(k, row, u_loc, v_all, weight)
        site_column = lax.dynamic_slice_in_dim(block, k, 1, 1)[:, 0] - jnp.dot(
            u_sites, v_site[0], precision=lax.Precision.HIGHEST
        )
        u_sites = lax.dynamic_update_slice_in_dim(u_sites, (coef * site_column)[:, None], k, 1)
        return (u_loc, v_all, weight, u_sites)

    u_loc, v_all, weight, u_sites = lax.fori_loop(
        0, steps, step, (u_start, v_start, w_start, jnp.zeros((steps, steps), jnp.float32))
    )
    updated = local - jnp.dot(u_loc, v_all.T, precision=lax.Precision.HIGHEST)
    total = lax.psum(weight, "cols")
    return (updated[None], total)


def solution(mesh):
    in_specs = (P("cols", "rows", None), P(), P(), P())
    out_specs = (P("cols", "rows", None), P())
    return jax.shard_map(
        on_device, mesh=mesh, in_specs=in_specs, out_specs=out_specs, check_vma=False
    )
```

profile of v0, /device:TPU:0, one launch (start us, length us, event | category | flops | bytes accessed | tf_op | source)
XLA Modules:
  0.0 490.0 jit_solution(5684229516232508071)
XLA Ops:
  7.9 2.9 gather_fusion.1
  11.7 5.6 %copy.11 = f32[256,4096]{0,1:T(8,128)} copy(f32[256,4096]{1,0:T(8,128)} %bitcast.80) | data formatting | bytes 8388608
  18.0 105.7 %all-reduce.2.cloned.1.call-done = f32[16,4096]{1,0:T(8,128)} async-done(((f32[16,4096]{1,0:T(8,128)}), f32[16,4096]{1,0:T(8,128)}) %all-reduce.2.cloned.1.call-update) | async-done | bytes 262160 | tf_op jit(solution)/shard_map/psum | solution.py:42
  123.7 1.5 copy.10
  125.9 1.5 broadcast_in_dim.54
  127.4 344.6 %while.20 = (s32[]{:T(128)}, f32[256,16]{0,1:T(8,128)S(1)}, f32[4096,16]{1,0:T(8,128)}, f32[]{:T(128)}, f32[16,16]{1,0:T(8,128)S(1)}, /*index=5*/f32[16]{0:T(128...) while((s32[]{:T(128)}, f32[256,16]{0,1:T(8,128)S(1)}, ...), condition=%wide.region_2.3_spmd.clone, body=%wide.region_1.2_spmd.clone.sunk | while | flops 855597 | bytes 2257639 | solution.py:57
  130.0 3.4 convolution_subtract_fusion.3
  137.8 0.8 fusion.40
  138.8 0.8 fusion.37
  142.4 5.8 %dynamic_update_slice.28 = f32[4096,16]{1,0:T(8,128)} dynamic-update-slice(f32[4096,16]{1,0:T(8,128)} %get-tuple-element.353, f32[4096,1]{1,0:T(8,128)S(1)} %copy.14, s32[]{:T(128)} %constant.100.clone.1..sunk, s32[]{:T(128)} %get-tuple-element.351) | dynamic-update-slice | bytes 32772 | tf_op jit(solution)/shard_map/while/body/eval_jaxpr/dynamic_update_slice | solution.py:33
  150.9 3.4 convolution_subtract_fusion.3
  158.6 0.8 fusion.40
  159.6 0.8 fusion.37
  163.2 6.5 %dynamic_update_slice.28 = f32[4096,16]{1,0:T(8,128)} dynamic-update-slice(f32[4096,16]{1,0:T(8,128)} %get-tuple-element.353, f32[4096,1]{1,0:T(8,128)S(1)} %copy.14, s32[]{:T(128)} %constant.100.clone.1..sunk, s32[]{:T(128)} %get-tuple-element.351) | dynamic-update-slice | bytes 32772 | tf_op jit(solution)/shard_map/while/body/eval_jaxpr/dynamic_update_slice | solution.py:33
  172.5 3.4 convolution_subtract_fusion.3
  180.2 0.8 fusion.40
  181.2 0.8 fusion.37
  184.8 6.5 %dynamic_update_slice.28 = f32[4096,16]{1,0:T(8,128)} dynamic-update-slice(f32[4096,16]{1,0:T(8,128)} %get-tuple-element.353, f32[4096,1]{1,0:T(8,128)S(1)} %copy.14, s32[]{:T(128)} %constant.100.clone.1..sunk, s32[]{:T(128)} %get-tuple-element.351) | dynamic-update-slice | bytes 32772 | tf_op jit(solution)/shard_map/while/body/eval_jaxpr/dynamic_update_slice | solution.py:33
  194.0 3.4 convolution_subtract_fusion.3
  202.8 0.8 fusion.37
  206.4 6.5 %dynamic_update_slice.28 = f32[4096,16]{1,0:T(8,128)} dynamic-update-slice(f32[4096,16]{1,0:T(8,128)} %get-tuple-element.353, f32[4096,1]{1,0:T(8,128)S(1)} %copy.14, s32[]{:T(128)} %constant.100.clone.1..sunk, s32[]{:T(128)} %get-tuple-element.351) | dynamic-update-slice | bytes 32772 | tf_op jit(solution)/shard_map/while/body/eval_jaxpr/dynamic_update_slice | solution.py:33
  215.6 3.4 convolution_subtract_fusion.3
  224.4 0.8 fusion.37
  228.0 6.5 %dynamic_update_slice.28 = f32[4096,16]{1,0:T(8,128)} dynamic-update-slice(f32[4096,16]{1,0:T(8,128)} %get-tuple-element.353, f32[4096,1]{1,0:T(8,128)S(1)} %copy.14, s32[]{:T(128)} %constant.100.clone.1..sunk, s32[]{:T(128)} %get-tuple-element.351) | dynamic-update-slice | bytes 32772 | tf_op jit(solution)/shard_map/while/body/eval_jaxpr/dynamic_update_slice | solution.py:33
  237.2 3.4 convolution_subtract_fusion.3
  245.0 0.8 fusion.40
  246.0 0.8 fusion.37
  249.6 6.5 %dynamic_update_slice.28 = f32[4096,16]{1,0:T(8,128)} dynamic-update-slice(f32[4096,16]{1,0:T(8,128)} %get-tuple-element.353, f32[4096,1]{1,0:T(8,128)S(1)} %copy.14, s32[]{:T(128)} %constant.100.clone.1..sunk, s32[]{:T(128)} %get-tuple-element.351) | dynamic-update-slice | bytes 32772 | tf_op jit(solution)/shard_map/while/body/eval_jaxpr/dynamic_update_slice | solution.py:33
  258.8 3.4 convolution_subtract_fusion.3
  267.5 0.8 fusion.37
  271.1 6.5 %dynamic_update_slice.28 = f32[4096,16]{1,0:T(8,128)} dynamic-update-slice(f32[4096,16]{1,0:T(8,128)} %get-tuple-element.353, f32[4096,1]{1,0:T(8,128)S(1)} %copy.14, s32[]{:T(128)} %constant.100.clone.1..sunk, s32[]{:T(128)} %get-tuple-element.351) | dynamic-update-slice | bytes 32772 | tf_op jit(solution)/shard_map/while/body/eval_jaxpr/dynamic_update_slice | solution.py:33
  280.4 3.4 convolution_subtract_fusion.3
  288.1 0.8 fusion.40
  289.1 0.8 fusion.37
  292.7 6.5 %dynamic_update_slice.28 = f32[4096,16]{1,0:T(8,128)} dynamic-update-slice(f32[4096,16]{1,0:T(8,128)} %get-tuple-element.353, f32[4096,1]{1,0:T(8,128)S(1)} %copy.14, s32[]{:T(128)} %constant.100.clone.1..sunk, s32[]{:T(128)} %get-tuple-element.351) | dynamic-update-slice | bytes 32772 | tf_op jit(solution)/shard_map/while/body/eval_jaxpr/dynamic_update_slice | solution.py:33
  301.9 3.4 convolution_subtract_fusion.3
  309.7 0.9 fusion.40
  310.7 0.9 fusion.37
  314.4 6.5 %dynamic_update_slice.28 = f32[4096,16]{1,0:T(8,128)} dynamic-update-slice(f32[4096,16]{1,0:T(8,128)} %get-tuple-element.353, f32[4096,1]{1,0:T(8,128)S(1)} %copy.14, s32[]{:T(128)} %constant.100.clone.1..sunk, s32[]{:T(128)} %get-tuple-element.351) | dynamic-update-slice | bytes 32772 | tf_op jit(solution)/shard_map/while/body/eval_jaxpr/dynamic_update_slice | solution.py:33
  323.6 3.4 convolution_subtract_fusion.3
  332.4 0.8 fusion.37
  335.9 6.5 %dynamic_update_slice.28 = f32[4096,16]{1,0:T(8,128)} dynamic-update-slice(f32[4096,16]{1,0:T(8,128)} %get-tuple-element.353, f32[4096,1]{1,0:T(8,128)S(1)} %copy.14, s32[]{:T(128)} %constant.100.clone.1..sunk, s32[]{:T(128)} %get-tuple-element.351) | dynamic-update-slice | bytes 32772 | tf_op jit(solution)/shard_map/while/body/eval_jaxpr/dynamic_update_slice | solution.py:33
  345.2 3.4 convolution_subtract_fusion.3
  353.9 0.8 fusion.37
  357.5 6.5 %dynamic_update_slice.28 = f32[4096,16]{1,0:T(8,128)} dynamic-update-slice(f32[4096,16]{1,0:T(8,128)} %get-tuple-element.353, f32[4096,1]{1,0:T(8,128)S(1)} %copy.14, s32[]{:T(128)} %constant.100.clone.1..sunk, s32[]{:T(128)} %get-tuple-element.351) | dynamic-update-slice | bytes 32772 | tf_op jit(solution)/shard_map/while/body/eval_jaxpr/dynamic_update_slice | solution.py:33
  366.7 3.4 convolution_subtract_fusion.3
  374.5 0.8 fusion.40
  375.5 0.8 fusion.37
  379.1 6.5 %dynamic_update_slice.28 = f32[4096,16]{1,0:T(8,128)} dynamic-update-slice(f32[4096,16]{1,0:T(8,128)} %get-tuple-element.353, f32[4096,1]{1,0:T(8,128)S(1)} %copy.14, s32[]{:T(128)} %constant.100.clone.1..sunk, s32[]{:T(128)} %get-tuple-element.351) | dynamic-update-slice | bytes 32772 | tf_op jit(solution)/shard_map/while/body/eval_jaxpr/dynamic_update_slice | solution.py:33
  388.3 3.4 convolution_subtract_fusion.3
  397.1 0.8 fusion.37
  400.7 6.5 %dynamic_update_slice.28 = f32[4096,16]{1,0:T(8,128)} dynamic-update-slice(f32[4096,16]{1,0:T(8,128)} %get-tuple-element.353, f32[4096,1]{1,0:T(8,128)S(1)} %copy.14, s32[]{:T(128)} %constant.100.clone.1..sunk, s32[]{:T(128)} %get-tuple-element.351) | dynamic-update-slice | bytes 32772 | tf_op jit(solution)/shard_map/while/body/eval_jaxpr/dynamic_update_slice | solution.py:33
  409.9 3.4 convolution_subtract_fusion.3
  418.7 0.8 fusion.37
  422.2 6.5 %dynamic_update_slice.28 = f32[4096,16]{1,0:T(8,128)} dynamic-update-slice(f32[4096,16]{1,0:T(8,128)} %get-tuple-element.353, f32[4096,1]{1,0:T(8,128)S(1)} %copy.14, s32[]{:T(128)} %constant.100.clone.1..sunk, s32[]{:T(128)} %get-tuple-element.351) | dynamic-update-slice | bytes 32772 | tf_op jit(solution)/shard_map/while/body/eval_jaxpr/dynamic_update_slice | solution.py:33
  431.5 3.4 convolution_subtract_fusion.3
  440.2 0.8 fusion.37
  443.8 6.5 %dynamic_update_slice.28 = f32[4096,16]{1,0:T(8,128)} dynamic-update-slice(f32[4096,16]{1,0:T(8,128)} %get-tuple-element.353, f32[4096,1]{1,0:T(8,128)S(1)} %copy.14, s32[]{:T(128)} %constant.100.clone.1..sunk, s32[]{:T(128)} %get-tuple-element.351) | dynamic-update-slice | bytes 32772 | tf_op jit(solution)/shard_map/while/body/eval_jaxpr/dynamic_update_slice | solution.py:33
  453.1 3.4 convolution_subtract_fusion.3
  460.8 0.8 fusion.40
  461.8 0.8 fusion.37
  465.4 6.5 %dynamic_update_slice.28 = f32[4096,16]{1,0:T(8,128)} dynamic-update-slice(f32[4096,16]{1,0:T(8,128)} %get-tuple-element.353, f32[4096,1]{1,0:T(8,128)S(1)} %copy.14, s32[]{:T(128)} %constant.100.clone.1..sunk, s32[]{:T(128)} %get-tuple-element.351) | dynamic-update-slice | bytes 32772 | tf_op jit(solution)/shard_map/while/body/eval_jaxpr/dynamic_update_slice | solution.py:33
  472.0 3.6 psum.15
  475.6 7.6 %fusion.14 = f32[1,256,4096]{2,1,0:T(8,128)} fusion(f32[256,16]{0,1:T(8,128)S(1)} %get-tuple-element.203, f32[4096,16]{1,0:T(8,128)} %get-tuple-element.204, f32[1,256,4096]{2,1,0:T(8,128)} %param.6), kind=kOutput, calls=%fused_computation.23 | convolution fusion | flops 202375168 | bytes 8667136 | tf_op jit(solution)/shard_map/dot_general | solution.py:60
  (204 shorter events, 85.3 us)
Async XLA Ops:
  7.2 10.2 %copy-start = (s32[4096]{0:T(1024)S(1)}, s32[4096]{0:T(1024)}, u32[]{:S(2)}) copy-start(s32[4096]{0:T(1024)} %param.8) | copy-start | bytes 49156
  7.2 4.5 copy-start.1
  7.2 116.5 %all-reduce.2.cloned.1.call-start = ((), (), s32[]{:S(2)}) async-start(), calls=%async_computation | async-start | bytes 524288 | tf_op jit(solution)/shard_map/psum | solution.py:42
  11.7 5.6 %copy-start.2 = (s32[16]{0:T(128)S(1)}, s32[16]{0:T(128)}, u32[]{:S(2)}) copy-start(s32[16]{0:T(128)} %param.9) | copy-start | bytes 196
Sparse Core Ops, SparseCore 0:
  13.2 110.4 all-reduce.1
where the time goes:
time: 496 us; the launch traced here: 490 us
  local copies, waits for them, and re-layouts  172 us (35%)
  waiting for transfers between devices  106 us (21%)
  matrix products  87.9 us (18%)
  loops' own time  84.3 us (17%)
  other arithmetic  22.5 us (5%)
  between operations  14.1 us (3%)
    psum x1, waiting for transfers between devices, on_device(): raw_rows = lax.psum(picked, 'rows')  106 us
    dynamic_update_slice x16, local copies, waits for them, and re-layouts, advance(): v_all = lax.dynamic_update_slice_in_dim(v_all, fresh.T, k, 1)  104 us
    another operation x1, loops' own time, on_device(): lax.fori_loop(0, steps, step, (u_start, v_start, w_start, jnp.zeros((step...  84.3 us
    dot_general x16, matrix products, step(): jnp.dot(lax.dynamic_slice_in_dim(u_sites, k, 1, 0), v_all.T, precision=la...  54.1 us
    dynamic_slice x32, local copies, waits for them, and re-layouts, advance(): coef = flags[k] * deltas[k] / ratio  19.9 us
    dot_general x16, matrix products, advance(): jnp.dot(u_loc, v_site[0], precision=lax.Precision.HIGHEST)  13.2 us
    dot_general x16, matrix products, step(): jnp.dot(u_sites, v_site[0], precision=lax.Precision.HIGHEST)  13 us
    dynamic_slice x16, local copies, waits for them, and re-layouts, advance(): lax.dynamic_slice_in_dim(local, site, 1, 1)[:, 0]  11.4 us
  transfers between devices with their start and end apart: 1, of which 1 were waited for; matrix products, arithmetic and copies ran while one was open for 1% of the time, Pallas kernels for 0%

commit v1 on v0

v1 whole, which is shorter than its diff:
```python
import functools

import jax
import jax.numpy as jnp
import numpy as np
from jax import lax
from jax.experimental import pallas as pl
from jax.experimental.pallas import tpu as pltpu
from jax.sharding import PartitionSpec as P

FLOOR = 0.25
COUPLING = 0.5
LANES = 128
MESH = pl.DeviceIdType.MESH


def pick_kernel(n, steps, rows_dev, width, cc, rg,
                sites_ref, fields_ref, accept_ref, local,
                picked, blk, spread_ref, site_ref, delta_ref, flag_ref):
    spin = lax.axis_index("cols")
    prow = steps // rg
    pcol = width // cc
    per = LANES // steps
    brow = steps // per
    first = lax.axis_index("rows") * rows_dev
    site = [sites_ref[k] for k in range(steps)]

    for k in range(steps):
        rel = site[k] - first
        inside = jnp.logical_and(rel >= 0, rel < rows_dev)
        row = local[pl.ds(jnp.clip(rel, 0, rows_dev - 1), 1), :]
        row = jnp.where(inside, row, 0.0)
        for c in range(cc):
            picked[(k // prow) * cc + c, k % prow:k % prow + 1, :] = row[:, c * pcol:(c + 1) * pcol]

    lane = lax.broadcasted_iota(jnp.int32, (steps, LANES), 1)
    sub = lax.broadcasted_iota(jnp.int32, (steps, LANES), 0)
    spread = jnp.zeros((rows_dev, LANES), jnp.float32)
    lane_c = lax.broadcasted_iota(jnp.int32, (rows_dev, LANES), 1)
    for j in range(steps):
        tile = pl.multiple_of((site[j] // LANES) * LANES, LANES)
        strip = local[:, pl.ds(tile, LANES)]
        value = jnp.sum(jnp.where(lane_c == site[j] - tile, strip, 0.0), axis=1, keepdims=True)
        spread = jnp.where(lane_c == j, value, spread)
    spread_ref[...] = spread

    block = jnp.zeros((steps, LANES), jnp.float32)
    sites_all = jnp.zeros((steps, LANES), jnp.int32)
    deltas = jnp.zeros((steps, LANES), jnp.float32)
    flags = jnp.zeros((steps, LANES), jnp.float32)
    same = np.float32(np.exp(np.float32(-2.0 * COUPLING))) - np.float32(1.0)
    differ = np.float32(np.exp(np.float32(2.0 * COUPLING))) - np.float32(1.0)
    for k in range(steps):
        rel = site[k] - first
        inside = jnp.logical_and(rel >= 0, rel < rows_dev)
        line = spread_ref[pl.ds(jnp.clip(rel, 0, rows_dev - 1), 1), :]
        line = jnp.where(inside, line, 0.0)
        block = jnp.where(sub == k, jnp.broadcast_to(line, block.shape), block)
        sites_all = jnp.where(sub == k, site[k], sites_all)
        delta = jnp.where(fields_ref[site[k]] == spin, same, differ)
        deltas = jnp.where(sub == k, delta, deltas)
        flags = jnp.where(sub == k, accept_ref[k].astype(jnp.float32), flags)
    site_ref[...] = sites_all
    delta_ref[...] = deltas
    flag_ref[...] = flags

    packed = []
    for q in range(brow):
        line = block[q * per:(q + 1) * per, :]
        sub_q = lax.broadcasted_iota(jnp.int32, (per, LANES), 0)
        acc = jnp.zeros((per, LANES), jnp.float32)
        for i in range(per):
            turned = line if i == 0 else pltpu.roll(line, i * steps, 1)
            acc = jnp.where(sub_q == i, turned, acc)
        packed.append(jnp.sum(acc, axis=0, keepdims=True))
    blk[...] = jnp.concatenate(packed, axis=0)


def exchange_kernel(n, steps, rows_dev, width, cc, rg,
                    picked, blk, spread_ref, site_ref, delta_ref, flag_ref,
                    ust_ref, vst_ref, total_ref,
                    landed, mine, raw, blks, wgt, wgt_in,
                    s1, r1, s2, r2, sb, rb, sw, rw):
    me = lax.axis_index("rows")
    other = 1 - lax.axis_index("cols")
    pcol = width // cc
    per = LANES // steps
    barrier = pltpu.get_barrier_semaphore()

    def greet(j, _):
        pl.semaphore_signal(barrier, inc=1, device_id={"rows": lax.rem(me + j, n)}, device_id_type=MESH)
        return _

    lax.fori_loop(1, n, greet, 0)
    pl.semaphore_signal(barrier, inc=1, device_id={"cols": other}, device_id_type=MESH)
    lane = lax.broadcasted_iota(jnp.int32, (steps, LANES), 1)
    sub = lax.broadcasted_iota(jnp.int32, (steps, LANES), 0)
    pl.semaphore_wait(barrier, n)

    def order(i):
        return 1 + lax.rem(i + n // 2 - 1, n - 1)

    def block_copy(j):
        to = lax.rem(me + j, n)
        return pltpu.make_async_remote_copy(
            src_ref=blk, dst_ref=blks.at[j], send_sem=sb.at[j], recv_sem=rb.at[j],
            device_id={"rows": to}, device_id_type=MESH)

    def first_copy(j):
        to = lax.rem(me + j, n)
        return pltpu.make_async_remote_copy(
            src_ref=picked.at[to], dst_ref=landed.at[j], send_sem=s1.at[j], recv_sem=r1.at[j],
            device_id={"rows": to}, device_id_type=MESH)

    def second_copy(j):
        to = lax.rem(me + j, n)
        return pltpu.make_async_remote_copy(
            src_ref=mine, dst_ref=raw.at[me], send_sem=s2.at[j], recv_sem=r2.at[j],
            device_id={"rows": to}, device_id_type=MESH)

    def each(fn):
        def body(i, _):
            fn(order(i))
            return _
        lax.fori_loop(0, n - 1, body, 0)

    each(lambda j: block_copy(j).start())
    each(lambda j: first_copy(j).start())

    each(lambda j: first_copy(j).wait_recv())
    chunk = picked[me]
    for j in range(1, n):
        chunk = chunk + landed[j]
    mine[...] = chunk
    raw[me] = chunk
    each(lambda j: second_copy(j).start())

    each(lambda j: block_copy(j).wait_recv())
    packed = blk[...]
    for j in range(1, n):
        packed = packed + blks[j]
    block = jnp.zeros((steps, LANES), jnp.float32)
    for k in range(steps):
        line = jnp.broadcast_to(packed[k // per:k // per + 1, :], (8, LANES))
        back = (LANES - (k % per) * steps) % LANES
        if back:
            line = pltpu.roll(line, back, 1)
        block = jnp.where(sub == k, jnp.broadcast_to(line[0:1, :], (steps, LANES)), block)
    one = jnp.float32(1.0)
    block = jnp.where(lane < steps, block, jnp.where(lane == sub + steps, one, 0.0))
    under = jnp.where(lane == sub, one, 0.0)
    z = jnp.concatenate([block, under], axis=0)
    lane_1 = lax.broadcasted_iota(jnp.int32, (1, LANES), 1)
    ratios = jnp.ones((1, LANES), jnp.float32)
    flags = jnp.zeros((1, LANES), jnp.float32)
    for k in range(steps):
        flag = flag_ref[k:k + 1, :]
        delta = delta_ref[k:k + 1, :]
        row = z[k:k + 1, :]
        column = jnp.broadcast_to(z[:, k:k + 1], z.shape)
        diag = column[k:k + 1, :]
        ratio = jnp.maximum(1.0 + delta * (1.0 - diag), FLOOR)
        coef = (flag * delta) / ratio
        fresh = jnp.where(lane_1 == k, one, 0.0) - row
        z = z - column * (coef * fresh)
        ratios = jnp.where(lane_1 == k, ratio, ratios)
        flags = jnp.where(lane_1 == k, flag, flags)
    weight = jnp.sum(flags * jnp.log(ratios), axis=1, keepdims=True)
    wgt[...] = jnp.broadcast_to(weight, (8, LANES))
    swap = pltpu.make_async_remote_copy(
        src_ref=wgt, dst_ref=wgt_in, send_sem=sw, recv_sem=rw,
        device_id={"cols": other}, device_id_type=MESH)
    swap.start()

    w = pltpu.roll(z[steps:2 * steps, :], LANES - steps, 1)
    w = jnp.where(lane < steps, w, 0.0)
    w = w + pltpu.roll(w, steps, 1) + pltpu.roll(w, 2 * steps, 1)
    w = jnp.concatenate([w, jnp.zeros((LANES - steps, LANES), jnp.float32)], axis=0)
    u = jnp.dot(spread_ref[...], w, precision=lax.Precision.HIGHEST, preferred_element_type=jnp.float32)
    lane_c = lax.broadcasted_iota(jnp.int32, (rows_dev, LANES), 1)
    high = u.astype(jnp.bfloat16).astype(jnp.float32)
    ust_ref[...] = jnp.where(lane_c < 2 * steps, high, u - high).astype(jnp.bfloat16)

    lane_p = lax.broadcasted_iota(jnp.int32, (steps, pcol), 1)
    owner = jnp.broadcast_to(site_ref[:, 0:1], (steps, pcol)) - lane_p

    each(lambda j: second_copy(j).wait_recv())
    for c in range(cc):
        parts = [raw[g * cc + c] for g in range(rg)]
        rows = parts[0] if rg == 1 else jnp.concatenate(parts, axis=0)
        v = jnp.where(owner == c * pcol, one, 0.0) - rows
        vh = v.astype(jnp.bfloat16)
        vl = (v - vh.astype(jnp.float32)).astype(jnp.bfloat16)
        vst_ref[:, c * pcol:(c + 1) * pcol] = jnp.concatenate([vh, vl, vh], axis=0)

    swap.wait()
    total_ref[0, 0] = jnp.max(wgt[0:1, :] + wgt_in[0:1, :])
    each(lambda j: block_copy(j).wait_send())
    each(lambda j: first_copy(j).wait_send())
    each(lambda j: second_copy(j).wait_send())


def apply_kernel(k3, tile, ust_ref, vst_ref, total_ref, local, out_ref, sum_ref):
    cols = pl.ds(pl.multiple_of(pl.program_id(0) * tile, tile), tile)
    out_ref[...] = local[:, cols] - jnp.dot(
        ust_ref[:, :k3], vst_ref[...], preferred_element_type=jnp.float32)
    sum_ref[0, 0] = total_ref[0, 0]


def on_device(n, green, sites, fields, accept):
    local = green[0]
    rows_dev, width = local.shape
    steps = sites.shape[0]
    cc = min(n, width // LANES)
    rg = n // cc
    brow = steps // (LANES // steps)
    prow, pcol = steps // rg, width // cc
    f32, i32, bf16 = jnp.float32, jnp.int32, jnp.bfloat16
    vmem = pl.BlockSpec(memory_space=pltpu.VMEM)
    smem = pl.BlockSpec(memory_space=pltpu.SMEM)
    dma = pltpu.SemaphoreType.DMA
    shape = jax.ShapeDtypeStruct
    limit = 16 * 1024 * 1024
    sizes = (n, steps, rows_dev, width, cc, rg)
    parts = pl.pallas_call(
        functools.partial(pick_kernel, *sizes),
        out_shape=(
            shape((n, prow, pcol), f32), shape((brow, LANES), f32), shape((rows_dev, LANES), f32),
            shape((steps, LANES), i32), shape((steps, LANES), f32), shape((steps, LANES), f32),
        ),
        in_specs=[smem, smem, smem, vmem],
        out_specs=(vmem,) * 6,
        compiler_params=pltpu.CompilerParams(vmem_limit_bytes=limit),
        cost_estimate=pl.CostEstimate(flops=10 ** 6, bytes_accessed=4 * rows_dev * width, transcendentals=0),
        name="pick",
    )(sites, fields, accept, local)

    ust, vst, total = pl.pallas_call(
        functools.partial(exchange_kernel, *sizes),
        out_shape=(shape((rows_dev, LANES), bf16), shape((3 * steps, width), bf16), shape((1, 1), f32)),
        in_specs=[vmem] * 6,
        out_specs=(vmem, vmem, smem),
        scratch_shapes=[
            pltpu.VMEM((n, prow, pcol), f32),
            pltpu.VMEM((prow, pcol), f32),
            pltpu.VMEM((n, prow, pcol), f32),
            pltpu.VMEM((n, brow, LANES), f32),
            pltpu.VMEM((8, LANES), f32),
            pltpu.VMEM((8, LANES), f32),
            dma((n,)), dma((n,)), dma((n,)), dma((n,)), dma((n,)), dma((n,)), dma, dma,
        ],
        compiler_params=pltpu.CompilerParams(
            collective_id=0, has_side_effects=True, vmem_limit_bytes=limit),
        cost_estimate=pl.CostEstimate(flops=10 ** 9, bytes_accessed=64 * 2 ** 20, transcendentals=0),
        name="exchange",
    )(*parts)

    tile = min(512, width)
    updated, summed = pl.pallas_call(
        functools.partial(apply_kernel, 3 * steps, tile),
        grid=(width // tile,),
        out_shape=(shape((rows_dev, width), f32), shape((1, 1), f32)),
        in_specs=[vmem, pl.BlockSpec((3 * steps, tile), lambda i: (0, i)), smem, vmem],
        out_specs=(pl.BlockSpec((rows_dev, tile), lambda i: (0, i)), smem),
        compiler_params=pltpu.CompilerParams(vmem_limit_bytes=limit),
        cost_estimate=pl.CostEstimate(
            flops=2 * rows_dev * width * 3 * steps, bytes_accessed=8 * rows_dev * width, transcendentals=0),
        name="apply",
    )(ust, vst, total, local)
    return updated[None], summed.reshape(())


def solution(mesh):
    in_specs = (P("cols", "rows", None), P(), P(), P())
    out_specs = (P("cols", "rows", None), P())
    return jax.shard_map(
        functools.partial(on_device, mesh.shape["rows"]),
        mesh=mesh, in_specs=in_specs, out_specs=out_specs, check_vma=False,
    )
```

time: 496 us -> 35.5 us (0.07); the launches traced: 490 us -> 35.2 us
  local copies, waits for them, and re-layouts: 172 us -> 4.21 us
  waiting for transfers between devices: 106 us -> 0 us
  matrix products: 87.9 us -> 0 us
  loops' own time: 84.3 us -> 0 us
  Pallas kernels: 0 us -> 30.4 us
  other arithmetic: 22.5 us -> 0 us
  between operations: 14.1 us -> 0.66 us
    dynamic_update_slice x48 -> x0, local copies, waits for them, and re-layouts: 106 us -> none  [the longest x16 104 us: advance(): v_all = lax.dynamic_update_slice_in_dim(v_all, fresh.T, k, 1)]
    psum x1 -> x0, waiting for transfers between devices: 106 us -> none  [on_device(): raw_rows = lax.psum(picked, 'rows')]
    dot_general x49 -> x0, matrix products: 87.9 us -> none  [the longest x16 54.1 us: step(): jnp.dot(lax.dynamic_slice_in_dim(u_sites, k, 1, 0), v_all.T, precision=la...]
    another operation x1 -> x0, loops' own time: 84.3 us -> none  [on_device(): lax.fori_loop(0, steps, step, (u_start, v_start, w_start, jnp.zeros((step...]
    dynamic_slice x64 -> x0, local copies, waits for them, and re-layouts: 41.7 us -> none  [the longest x32 19.9 us: advance(): coef = flags[k] * deltas[k] / ratio]
    pallas_call x0 -> x3, Pallas kernels: none -> 30.4 us  [the longest x1 23.9 us: on_device(): pl.pallas_call(functools.partial(exchange_kernel, *sizes), out_shape=(sha...]
    transpose x16 -> x0, other arithmetic: 11.1 us -> none  [advance(): v_all = lax.dynamic_update_slice_in_dim(v_all, fresh.T, k, 1)]
    transpose x16 -> x0, local copies, waits for them, and re-layouts: 10.2 us -> none  [advance(): v_all = lax.dynamic_update_slice_in_dim(v_all, fresh.T, k, 1)]
  transfers between devices with their start and end apart: 1 -> 0, of which waited for: 1 -> 0; matrix products, arithmetic and copies ran while one was open for 1% -> 0% of each run, Pallas kernels for 0% -> 0%
where the time goes in v1:
time: 35.5 us; the launch traced here: 35.2 us
  Pallas kernels  30.4 us (86%)
  local copies, waits for them, and re-layouts  4.21 us (12%)
  between operations  0.66 us (2%)
    pallas_call x1, Pallas kernels, on_device(): pl.pallas_call(functools.partial(exchange_kernel, *sizes), out_shape=(sha...  23.9 us
    pallas_call x1, Pallas kernels, on_device(): pl.pallas_call(functools.partial(apply_kernel, 3 * steps, tile), grid=(wi...  4.83 us
    unnamed x10, local copies, waits for them, and re-layouts  4.21 us
    pallas_call x1, Pallas kernels, on_device(): pl.pallas_call(functools.partial(pick_kernel, *sizes), out_shape=(shape((...  1.66 us

profile of v1, /device:TPU:0, one launch (start us, length us, event | category | flops | bytes accessed | tf_op | source)
XLA Modules:
  0.0 35.2 jit_solution(6399018937637822938)
XLA Ops:
  0.6 0.0 copy-start
  0.6 2.2 %copy-done = f32[1,256,4096]{2,1,0:T(8,128)S(1)} copy-done((f32[1,256,4096]{2,1,0:T(8,128)S(1)}, f32[1,256,4096]{2,1,0:T(8,128)}, u32[]{:S(2)}) %copy-start) | copy-done | bytes 4194328
  2.8 0.0 copy-start.2
  2.8 0.7 %copy-done.2 = s32[4096]{0:T(1024)S(1)} copy-done((s32[4096]{0:T(1024)S(1)}, s32[4096]{0:T(1024)}, u32[]{:S(2)}) %copy-start.2) | copy-done | bytes 16408
  3.5 0.0 copy-start.3
  3.5 0.7 %copy-done.3 = s32[16]{0:T(128)S(1)} copy-done((s32[16]{0:T(128)S(1)}, s32[16]{0:T(128)}, u32[]{:S(2)}) %copy-start.3) | copy-done | bytes 88
  4.2 0.0 copy-start.4
  4.2 0.7 %copy-done.4 = s32[16]{0:T(128)S(1)} copy-done((s32[16]{0:T(128)S(1)}, s32[16]{0:T(128)}, u32[]{:S(2)}) %copy-start.4) | copy-done | bytes 88
  4.8 0.0 copy-start.1
  4.9 1.7 %pick.1 = (f32[16,16,256]{2,1,0:T(8,128)S(1)}, f32[2,128]{1,0:T(2,128)S(1)}, f32[256,128]{1,0:T(8,128)S(1)}, s32[16,128]{1,0:T(8,128)S(1)}, f32[16,128]{1,0:T(8,128)S(1)}, /*index=5*/f32[16,128]{1,0:T(8,128)S(1)}) custom-call(s32[16]{0:T(128)S(1)} %copy-done.3, s32[4096]{0:T(1024)S(1)} %copy-done.2, s32[16]{0:T(128)S(1)} %copy-done.4, f32[256,4096]{1,0:T(8,128)S(1)} %bitcast.3), custom_call_target="tpu_custom_call" | custom-call | flops 1000000 | bytes 4194304 | tf_op jit(solution)/shard_map/pick/pallas_call | solution.py:225
  6.5 23.9 %exchange.1 = (bf16[256,128]{1,0:T(8,128)(2,1)S(1)}, bf16[48,4096]{1,0:T(8,128)(2,1)S(1)}, f32[1,1]{1,0:T(1,128)}) custom-call(f32[16,16,256]{2,1,0:T(8,128)S(1)} %get-tuple-element.13.picked, f32[2,128]{1,0:T(2,128)S(1)} %get-tuple-element.14.blk, f32[256,128]{1,0:T(8,128)S(1)} %get-tuple-element.15.spread_ref, s32[16,128]{1,0:T(8,128)S(1)} %get-tuple-element.16.site_ref, ...), custom_call_target="tpu_custom_call" | custom-call | flops 1000000000 | bytes 67108864 | tf_op jit(solution)/shard_map/exchange/pallas_call | solution.py:238
  30.4 0.0 copy-done.1
  30.4 4.8 %apply.1 = (f32[256,4096]{1,0:T(8,128)}, f32[1,1]{1,0:T(1,128)}) custom-call(bf16[256,128]{1,0:T(8,128)(2,1)S(1)} %get-tuple-element.19.ust_ref, bf16[48,4096]{1,0:T(8,128)(2,1)S(1)} %get-tuple-element.20.vst_ref, f32[1,1]{1,0:T(1,128)} %get-tuple-element.21.total_ref, f32[256,4096]{1,0:T(8,128)S(1)} %bitcast.4), custom_call_target="tpu_custom_call" | custom-call | flops 100663296 | bytes 8388608 | tf_op jit(solution)/shard_map/apply/pallas_call | solution.py:259
Async XLA Ops:
  0.6 2.2 %copy-start = (f32[1,256,4096]{2,1,0:T(8,128)S(1)}, f32[1,256,4096]{2,1,0:T(8,128)}, u32[]{:S(2)}) copy-start(f32[1,256,4096]{2,1,0:T(8,128)} %param.4) | copy-start | bytes 12582916
  2.8 0.7 %copy-start.2 = (s32[4096]{0:T(1024)S(1)}, s32[4096]{0:T(1024)}, u32[]{:S(2)}) copy-start(s32[4096]{0:T(1024)} %fields_ref.1) | copy-start | bytes 49156
  3.5 0.7 %copy-start.3 = (s32[16]{0:T(128)S(1)}, s32[16]{0:T(128)}, u32[]{:S(2)}) copy-start(s32[16]{0:T(128)} %sites_ref.1) | copy-start | bytes 196
  4.2 0.7 %copy-start.4 = (s32[16]{0:T(128)S(1)}, s32[16]{0:T(128)}, u32[]{:S(2)}) copy-start(s32[16]{0:T(128)} %accept_ref.1) | copy-start | bytes 196
  4.8 25.6 %copy-start.1 = (f32[1,256,4096]{2,1,0:T(8,128)S(1)}, f32[1,256,4096]{2,1,0:T(8,128)}, u32[]{:S(2)}) copy-start(f32[1,256,4096]{2,1,0:T(8,128)} %param.4) | copy-start | bytes 12582916

commit v2 on v1

v2 whole, which is shorter than its diff:
```python
import functools

import jax
import jax.numpy as jnp
import numpy as np
from jax import lax
from jax.experimental import pallas as pl
from jax.experimental.pallas import tpu as pltpu
from jax.sharding import PartitionSpec as P

FLOOR = 0.25
COUPLING = 0.5
LANES = 128
MESH = pl.DeviceIdType.MESH


def exchange_kernel(n, steps, rows_dev, width, cc, rg,
                    sites_hbm, fields_hbm, accept_hbm, green_hbm,
                    ust_ref, vst_ref, total_ref,
                    sites_ref, fields_ref, accept_ref, local, picked, spread_ref,
                    landed, mine, raw, blk, blks, wgt, wgt_in,
                    ls, s1, r1, s2, r2, sb, rb, sw, rw):
    me = lax.axis_index("rows")
    spin = lax.axis_index("cols")
    other = 1 - spin
    prow = steps // rg
    pcol = width // cc
    per = LANES // steps
    brow = steps // per

    loads = [
        pltpu.make_async_copy(sites_hbm, sites_ref, ls.at[0]),
        pltpu.make_async_copy(accept_hbm, accept_ref, ls.at[1]),
        pltpu.make_async_copy(fields_hbm, fields_ref, ls.at[2]),
        pltpu.make_async_copy(green_hbm, local, ls.at[3]),
    ]
    for load in loads:
        load.start()

    barrier = pltpu.get_barrier_semaphore()

    def greet(j, _):
        pl.semaphore_signal(barrier, inc=1, device_id={"rows": lax.rem(me + j, n)}, device_id_type=MESH)
        return _

    lax.fori_loop(1, n, greet, 0)
    pl.semaphore_signal(barrier, inc=1, device_id={"cols": other}, device_id_type=MESH)

    first = me * rows_dev
    for load in loads:
        load.wait()
    site = [sites_ref[k] for k in range(steps)]
    lane = lax.broadcasted_iota(jnp.int32, (steps, LANES), 1)
    sub = lax.broadcasted_iota(jnp.int32, (steps, LANES), 0)
    lane_1 = lax.broadcasted_iota(jnp.int32, (1, LANES), 1)

    span = min(2 * LANES, width)
    site_sub = jnp.zeros((steps, rows_dev), jnp.int32)
    row_at = lax.broadcasted_iota(jnp.int32, (steps, rows_dev), 0)
    for k in range(steps):
        site_sub = jnp.where(row_at == k, site[k], site_sub)
    mark = lax.broadcasted_iota(jnp.int32, (steps, rows_dev), 1) + first
    chosen = jnp.where(site_sub == mark, 1.0, 0.0).astype(jnp.bfloat16)

    def split(x):
        h = x.astype(jnp.bfloat16)
        rest = x - h.astype(jnp.float32)
        m = rest.astype(jnp.bfloat16)
        return h, m, (rest - m.astype(jnp.float32)).astype(jnp.bfloat16)

    def mul(x, y):
        return jnp.dot(x, y, preferred_element_type=jnp.float32)

    for q in range(width // span):
        h, m, l = split(local[:, q * span:(q + 1) * span])
        got = mul(chosen, h) + mul(chosen, m) + mul(chosen, l)
        for t in range(span // LANES):
            p, o = divmod(q * span + t * LANES, pcol)
            for g in range(rg):
                picked[g * cc + p, :, o:o + LANES] = got[g * prow:(g + 1) * prow, t * LANES:(t + 1) * LANES]

    pl.semaphore_wait(barrier, n)

    def order(i):
        return 1 + lax.rem(i + n // 2 - 1, n - 1)

    def block_copy(j):
        to = lax.rem(me + j, n)
        return pltpu.make_async_remote_copy(
            src_ref=blk, dst_ref=blks.at[j], send_sem=sb.at[j], recv_sem=rb.at[j],
            device_id={"rows": to}, device_id_type=MESH)

    def first_copy(j):
        to = lax.rem(me + j, n)
        return pltpu.make_async_remote_copy(
            src_ref=picked.at[to], dst_ref=landed.at[j], send_sem=s1.at[j], recv_sem=r1.at[j],
            device_id={"rows": to}, device_id_type=MESH)

    def second_copy(j):
        to = lax.rem(me + j, n)
        return pltpu.make_async_remote_copy(
            src_ref=mine, dst_ref=raw.at[me], send_sem=s2.at[j], recv_sem=r2.at[j],
            device_id={"rows": to}, device_id_type=MESH)

    def each(fn):
        def body(i, _):
            fn(order(i))
            return _
        lax.fori_loop(0, n - 1, body, 0)

    each(lambda j: first_copy(j).start())

    site_lane = jnp.full((span, LANES), -1, jnp.int32)
    lane_s = lax.broadcasted_iota(jnp.int32, (span, LANES), 1)
    for k in range(steps):
        site_lane = jnp.where(lane_s == k, site[k], site_lane)
    site_lane = site_lane - lax.broadcasted_iota(jnp.int32, (span, LANES), 0)
    block = jnp.zeros((steps, LANES), jnp.float32)
    for q in range(width // span):
        wanted = jnp.where(site_lane == q * span, 1.0, 0.0).astype(jnp.bfloat16)
        pieces = []
        for t in range(span // LANES):
            p, o = divmod(q * span + t * LANES, pcol)
            parts = [picked[g * cc + p, :, o:o + LANES] for g in range(rg)]
            pieces.append(parts[0] if rg == 1 else jnp.concatenate(parts, axis=0))
        h, m, l = split(jnp.concatenate(pieces, axis=1))
        block = block + (mul(h, wanted) + mul(m, wanted) + mul(l, wanted))
    packed = []
    for q in range(brow):
        line = block[q * per:(q + 1) * per, :]
        sub_q = lax.broadcasted_iota(jnp.int32, (per, LANES), 0)
        acc = jnp.zeros((per, LANES), jnp.float32)
        for i in range(per):
            turned = line if i == 0 else pltpu.roll(line, i * steps, 1)
            acc = jnp.where(sub_q == i, turned, acc)
        packed.append(jnp.sum(acc, axis=0, keepdims=True))
    blk[...] = jnp.concatenate(packed, axis=0)
    each(lambda j: block_copy(j).start())

    spread = jnp.zeros((rows_dev, LANES), jnp.float32)
    lane_c = lax.broadcasted_iota(jnp.int32, (rows_dev, LANES), 1)
    for q in range(width // span):
        wanted = jnp.where(site_lane == q * span, 1.0, 0.0).astype(jnp.bfloat16)
        h, m, l = split(local[:, q * span:(q + 1) * span])
        spread = spread + (mul(h, wanted) + mul(m, wanted) + mul(l, wanted))
    spread_ref[...] = spread

    each(lambda j: first_copy(j).wait_recv())
    chunk = picked[me]
    for j in range(1, n):
        chunk = chunk + landed[j]
    mine[...] = chunk
    raw[me] = chunk
    each(lambda j: second_copy(j).start())

    each(lambda j: block_copy(j).wait_recv())
    packed = blk[...]
    for j in range(1, n):
        packed = packed + blks[j]
    block = jnp.zeros((steps, LANES), jnp.float32)
    for k in range(steps):
        line = jnp.broadcast_to(packed[k // per:k // per + 1, :], (8, LANES))
        back = (LANES - (k % per) * steps) % LANES
        if back:
            line = pltpu.roll(line, back, 1)
        block = jnp.where(sub == k, jnp.broadcast_to(line[0:1, :], (steps, LANES)), block)
    one = jnp.float32(1.0)
    block = jnp.where(lane < steps, block, jnp.where(lane == sub + steps, one, 0.0))
    under = jnp.where(lane == sub, one, 0.0)
    z = jnp.concatenate([block, under], axis=0)
    same = np.float32(np.exp(np.float32(-2.0 * COUPLING))) - np.float32(1.0)
    differ = np.float32(np.exp(np.float32(2.0 * COUPLING))) - np.float32(1.0)
    fields = fields_ref[...]
    place = (lax.broadcasted_iota(jnp.int32, fields.shape, 0) * LANES
             + lax.broadcasted_iota(jnp.int32, fields.shape, 1))
    deltas = []
    for k in range(steps):
        found = jnp.where(place == site[k], fields.astype(jnp.float32), 0.0)
        found = jnp.sum(jnp.sum(found, axis=0, keepdims=True), axis=1, keepdims=True)
        found = jnp.broadcast_to(found, (1, LANES)) * jnp.ones((1, LANES), jnp.float32)
        kind = jnp.where(spin + 0 * lane_1 == 0, found, 1.0 - found)
        deltas.append(same + kind * (differ - same))
    ratios = jnp.ones((1, LANES), jnp.float32)
    flags = jnp.zeros((1, LANES), jnp.float32)
    for k in range(steps):
        flag = accept_ref[k].astype(jnp.float32)
        delta = deltas[k]
        row = z[k:k + 1, :]
        column = jnp.broadcast_to(z[:, k:k + 1], z.shape)
        diag = column[k:k + 1, :]
        ratio = jnp.maximum(1.0 + delta * (1.0 - diag), FLOOR)
        coef = (flag * delta) / ratio
        fresh = jnp.where(lane_1 == k, one, 0.0) - row
        z = z - column * (coef * fresh)
        ratios = jnp.where(lane_1 == k, ratio, ratios)
        flags = jnp.where(lane_1 == k, flag, flags)
    weight = jnp.sum(flags * jnp.log(ratios), axis=1, keepdims=True)
    wgt[...] = jnp.broadcast_to(weight, (8, LANES))
    swap = pltpu.make_async_remote_copy(
        src_ref=wgt, dst_ref=wgt_in, send_sem=sw, recv_sem=rw,
        device_id={"cols": other}, device_id_type=MESH)
    swap.start()

    w = pltpu.roll(z[steps:2 * steps, :], LANES - steps, 1)
    w = jnp.where(lane < steps, w, 0.0)
    w = w + pltpu.roll(w, steps, 1) + pltpu.roll(w, 2 * steps, 1)
    w = jnp.concatenate([w, jnp.zeros((LANES - steps, LANES), jnp.float32)], axis=0)
    u = jnp.dot(spread_ref[...], w, precision=lax.Precision.HIGHEST, preferred_element_type=jnp.float32)
    high = u.astype(jnp.bfloat16).astype(jnp.float32)
    ust_ref[...] = jnp.where(lane_c < 2 * steps, high, u - high).astype(jnp.bfloat16)

    lane_p = lax.broadcasted_iota(jnp.int32, (steps, pcol), 1)
    sub_p = lax.broadcasted_iota(jnp.int32, (steps, pcol), 0)
    owner = jnp.zeros((steps, pcol), jnp.int32)
    for k in range(steps):
        owner = jnp.where(sub_p == k, site[k], owner)
    owner = owner - lane_p

    each(lambda j: second_copy(j).wait_recv())
    for c in range(cc):
        parts = [raw[g * cc + c] for g in range(rg)]
        rows = parts[0] if rg == 1 else jnp.concatenate(parts, axis=0)
        v = jnp.where(owner == c * pcol, one, 0.0) - rows
        vh = v.astype(jnp.bfloat16)
        vl = (v - vh.astype(jnp.float32)).astype(jnp.bfloat16)
        vst_ref[:, c * pcol:(c + 1) * pcol] = jnp.concatenate([vh, vl, vh], axis=0)

    swap.wait()
    total_ref[0, 0] = jnp.max(wgt[0:1, :] + wgt_in[0:1, :])
    each(lambda j: block_copy(j).wait_send())
    each(lambda j: first_copy(j).wait_send())
    each(lambda j: second_copy(j).wait_send())


def apply_kernel(k3, tile, ust_ref, vst_ref, total_ref, local, out_hbm, sum_ref, held, sems):
    copies = []
    ust = ust_ref[:, :k3]
    for i in range(local.shape[1] // tile):
        cols = slice(i * tile, (i + 1) * tile)
        held[:, cols] = local[:, cols] - jnp.dot(
            ust, vst_ref[:, cols], preferred_element_type=jnp.float32)
        copies.append(pltpu.make_async_copy(held.at[:, cols], out_hbm.at[:, cols], sems.at[i]))
        copies[-1].start()
    sum_ref[0, 0] = total_ref[0, 0]
    for copy in copies:
        copy.wait()


def on_device(n, green, sites, fields, accept):
    local = green[0]
    rows_dev, width = local.shape
    steps = sites.shape[0]
    cc = min(n, width // LANES)
    rg = n // cc
    brow = steps // (LANES // steps)
    prow, pcol = steps // rg, width // cc
    f32, i32, bf16 = jnp.float32, jnp.int32, jnp.bfloat16
    vmem = pl.BlockSpec(memory_space=pltpu.VMEM)
    smem = pl.BlockSpec(memory_space=pltpu.SMEM)
    dma = pltpu.SemaphoreType.DMA
    shape = jax.ShapeDtypeStruct
    limit = 16 * 1024 * 1024
    sizes = (n, steps, rows_dev, width, cc, rg)
    ust, vst, total = pl.pallas_call(
        functools.partial(exchange_kernel, *sizes),
        out_shape=(shape((rows_dev, LANES), bf16), shape((3 * steps, width), bf16), shape((1, 1), f32)),
        in_specs=[pl.BlockSpec(memory_space=pltpu.HBM)] * 4,
        out_specs=(vmem, vmem, smem),
        scratch_shapes=[
            pltpu.SMEM((steps,), i32),
            pltpu.VMEM((fields.shape[0] // LANES, LANES), i32),
            pltpu.SMEM((steps,), i32),
            pltpu.VMEM((rows_dev, width), f32),
            pltpu.VMEM((n, prow, pcol), f32),
            pltpu.VMEM((rows_dev, LANES), f32),
            pltpu.VMEM((n, prow, pcol), f32),
            pltpu.VMEM((prow, pcol), f32),
            pltpu.VMEM((n, prow, pcol), f32),
            pltpu.VMEM((brow, LANES), f32),
            pltpu.VMEM((n, brow, LANES), f32),
            pltpu.VMEM((8, LANES), f32),
            pltpu.VMEM((8, LANES), f32),
            dma((4,)), dma((n,)), dma((n,)), dma((n,)), dma((n,)), dma((n,)), dma((n,)), dma, dma,
        ],
        compiler_params=pltpu.CompilerParams(
            collective_id=0, has_side_effects=True, vmem_limit_bytes=54 * 1024 * 1024),
        cost_estimate=pl.CostEstimate(flops=10 ** 9, bytes_accessed=64 * 2 ** 20, transcendentals=0),
        name="exchange",
    )(sites, fields.reshape(-1, LANES), accept, local)

    tile = min(512, width)
    updated, summed = pl.pallas_call(
        functools.partial(apply_kernel, 3 * steps, tile),
        out_shape=(shape((rows_dev, width), f32), shape((1, 1), f32)),
        in_specs=[vmem, vmem, smem, vmem],
        out_specs=(pl.BlockSpec(memory_space=pltpu.HBM), smem),
        scratch_shapes=[pltpu.VMEM((rows_dev, width), f32), dma((width // tile,))],
        compiler_params=pltpu.CompilerParams(vmem_limit_bytes=limit),
        cost_estimate=pl.CostEstimate(
            flops=2 * rows_dev * width * 3 * steps, bytes_accessed=8 * rows_dev * width, transcendentals=0),
        name="apply",
    )(ust, vst, total, local)
    return updated[None], summed.reshape(())


def solution(mesh):
    in_specs = (P("cols", "rows", None), P(), P(), P())
    out_specs = (P("cols", "rows", None), P())
    return jax.shard_map(
        functools.partial(on_device, mesh.shape["rows"]),
        mesh=mesh, in_specs=in_specs, out_specs=out_specs, check_vma=False,
    )
```

time: 35.5 us -> 30.1 us (0.85)
  Pallas kernels: 30.4 us -> 27.4 us
  local copies, waits for them, and re-layouts: 4.21 us -> 1.83 us
    pallas_call x2 -> x1, Pallas kernels: 6.49 us -> 3.36 us  [on_device(): pl.pallas_call(functools.partial(apply_kernel, 3 * steps, tile), out_shap...]
    unnamed x10 -> x6, local copies, waits for them, and re-layouts: 4.21 us -> 1.83 us
where the time goes in v2:
time: 30.1 us; the launch traced here: 29.9 us
  Pallas kernels  27.4 us (91%)
  local copies, waits for them, and re-layouts  1.83 us (6%)
  between operations  0.66 us (2%)
    pallas_call x1, Pallas kernels, on_device(): pl.pallas_call(functools.partial(exchange_kernel, *sizes), out_shape=(sha...  24.1 us
    pallas_call x1, Pallas kernels, on_device(): pl.pallas_call(functools.partial(apply_kernel, 3 * steps, tile), out_shap...  3.36 us
    unnamed x6, local copies, waits for them, and re-layouts  1.83 us

profile of v2, /device:TPU:0, one launch (start us, length us, event | category | flops | bytes accessed | tf_op | source)
XLA Modules:
  0.0 29.9 jit_solution(11891685241959614906)
XLA Ops:
  0.6 0.0 copy-start
  0.6 24.1 %exchange.1 = (bf16[256,128]{1,0:T(8,128)(2,1)}, bf16[48,4096]{1,0:T(8,128)(2,1)}, f32[1,1]{1,0:T(1,128)}) custom-call(s32[16]{0:T(128)} %sites_hbm.1, s32[32,128]{1,0:T(8,128)} %bitcast.6, s32[16]{0:T(128)} %accept_hbm.1, f32[256,4096]{1,0:T(8,128)} %bitcast.4), custom_call_target="tpu_custom_call" | custom-call | flops 1000000000 | bytes 67108864 | tf_op jit(solution)/shard_map/exchange/pallas_call | solution.py:264
  24.7 0.0 copy-done
  24.7 0.0 copy-start.1
  24.7 1.0 %copy-done.1 = bf16[48,4096]{1,0:T(8,128)(2,1)S(1)} copy-done((bf16[48,4096]{1,0:T(8,128)(2,1)S(1)}, bf16[48,4096]{1,0:T(8,128)(2,1)}, u32[]{:S(2)}) %copy-start.1) | copy-done | bytes 393240
  25.7 0.0 copy-start.2
  25.7 0.8 %copy-done.2 = bf16[256,128]{1,0:T(8,128)(2,1)S(1)} copy-done((bf16[256,128]{1,0:T(8,128)(2,1)S(1)}, bf16[256,128]{1,0:T(8,128)(2,1)}, u32[]{:S(2)}) %copy-start.2) | copy-done | bytes 65560
  26.6 3.4 %apply.1 = (f32[256,4096]{1,0:T(8,128)}, f32[1,1]{1,0:T(1,128)}) custom-call(bf16[256,128]{1,0:T(8,128)(2,1)S(1)} %copy-done.2, bf16[48,4096]{1,0:T(8,128)(2,1)S(1)} %copy-done.1, f32[1,1]{1,0:T(1,128)} %get-tuple-element.9.total_ref, f32[256,4096]{1,0:T(8,128)S(1)} %bitcast.5), custom_call_target="tpu_custom_call" | custom-call | flops 100663296 | bytes 8388608 | tf_op jit(solution)/shard_map/apply/pallas_call | solution.py:292
Async XLA Ops:
  0.6 24.1 %copy-start = (f32[1,256,4096]{2,1,0:T(8,128)S(1)}, f32[1,256,4096]{2,1,0:T(8,128)}, u32[]{:S(2)}) copy-start(f32[1,256,4096]{2,1,0:T(8,128)} %param.4) | copy-start | bytes 12582916
  24.7 1.0 %copy-start.1 = (bf16[48,4096]{1,0:T(8,128)(2,1)S(1)}, bf16[48,4096]{1,0:T(8,128)(2,1)}, u32[]{:S(2)}) copy-start(bf16[48,4096]{1,0:T(8,128)(2,1)} %get-tuple-element.8.vst_ref) | copy-start | bytes 1179652
  25.7 0.8 %copy-start.2 = (bf16[256,128]{1,0:T(8,128)(2,1)S(1)}, bf16[256,128]{1,0:T(8,128)(2,1)}, u32[]{:S(2)}) copy-start(bf16[256,128]{1,0:T(8,128)(2,1)} %get-tuple-element.7.ust_ref) | copy-start | bytes 196612

commit v3 on v2

--- a/solution.py
+++ b/solution.py
@@ -16,7 +16,7 @@
 
 def exchange_kernel(n, steps, rows_dev, width, cc, rg,
                     sites_hbm, fields_hbm, accept_hbm, green_hbm,
-                    ust_ref, vst_ref, total_ref,
+                    vst_ref, total_ref,
                     sites_ref, fields_ref, accept_ref, local, picked, spread_ref,
                     landed, mine, raw, blk, blks, wgt, wgt_in,
                     ls, s1, r1, s2, r2, sb, rb, sw, rw):
@@ -207,7 +207,10 @@
     w = jnp.concatenate([w, jnp.zeros((LANES - steps, LANES), jnp.float32)], axis=0)
     u = jnp.dot(spread_ref[...], w, precision=lax.Precision.HIGHEST, preferred_element_type=jnp.float32)
     high = u.astype(jnp.bfloat16).astype(jnp.float32)
-    ust_ref[...] = jnp.where(lane_c < 2 * steps, high, u - high).astype(jnp.bfloat16)
+    left = jnp.where(lane_c < 2 * steps, high, u - high).astype(jnp.bfloat16)
+    for g in range(-(-rows_dev // (3 * steps))):
+        part = left[g * 3 * steps:(g + 1) * 3 * steps, :]
+        vst_ref[:part.shape[0], width + g * LANES:width + (g + 1) * LANES] = part
 
     lane_p = lax.broadcasted_iota(jnp.int32, (steps, pcol), 1)
     sub_p = lax.broadcasted_iota(jnp.int32, (steps, pcol), 0)
@@ -232,9 +235,12 @@
     each(lambda j: second_copy(j).wait_send())
 
 
-def apply_kernel(k3, tile, ust_ref, vst_ref, total_ref, local, out_hbm, sum_ref, held, sems):
+def apply_kernel(k3, tile, vst_ref, total_ref, local, out_hbm, sum_ref, held, sems):
     copies = []
-    ust = ust_ref[:, :k3]
+    rows_dev, width = local.shape
+    groups = [vst_ref[:min(k3, rows_dev - g * k3), width + g * LANES:width + (g + 1) * LANES]
+              for g in range(-(-rows_dev // k3))]
+    ust = (groups[0] if len(groups) == 1 else jnp.concatenate(groups, axis=0))[:, :k3]
     for i in range(local.shape[1] // tile):
         cols = slice(i * tile, (i + 1) * tile)
         held[:, cols] = local[:, cols] - jnp.dot(
@@ -261,11 +267,12 @@
     shape = jax.ShapeDtypeStruct
     limit = 16 * 1024 * 1024
     sizes = (n, steps, rows_dev, width, cc, rg)
-    ust, vst, total = pl.pallas_call(
+    groups = -(-rows_dev // (3 * steps))
+    vst, total = pl.pallas_call(
         functools.partial(exchange_kernel, *sizes),
-        out_shape=(shape((rows_dev, LANES), bf16), shape((3 * steps, width), bf16), shape((1, 1), f32)),
+        out_shape=(shape((3 * steps, width + groups * LANES), bf16), shape((1, 1), f32)),
         in_specs=[pl.BlockSpec(memory_space=pltpu.HBM)] * 4,
-        out_specs=(vmem, vmem, smem),
+        out_specs=(vmem, smem),
         scratch_shapes=[
             pltpu.SMEM((steps,), i32),
             pltpu.VMEM((fields.shape[0] // LANES, LANES), i32),
@@ -292,14 +299,14 @@
     updated, summed = pl.pallas_call(
         functools.partial(apply_kernel, 3 * steps, tile),
         out_shape=(shape((rows_dev, width), f32), shape((1, 1), f32)),
-        in_specs=[vmem, vmem, smem, vmem],
+        in_specs=[vmem, smem, vmem],
         out_specs=(pl.BlockSpec(memory_space=pltpu.HBM), smem),
         scratch_shapes=[pltpu.VMEM((rows_dev, width), f32), dma((width // tile,))],
         compiler_params=pltpu.CompilerParams(vmem_limit_bytes=limit),
         cost_estimate=pl.CostEstimate(
             flops=2 * rows_dev * width * 3 * steps, bytes_accessed=8 * rows_dev * width, transcendentals=0),
         name="apply",
-    )(ust, vst, total, local)
+    )(vst, total, local)
     return updated[None], summed.reshape(())
 
 

time: 30.1 us -> 29.3 us (0.973)
  local copies, waits for them, and re-layouts: 1.83 us -> 1.02 us
    unnamed x6 -> x4, local copies, waits for them, and re-layouts: 1.83 us -> 1.02 us
where the time goes in v3:
time: 29.3 us; the launch traced here: 29.1 us
  Pallas kernels  27.4 us (94%)
  local copies, waits for them, and re-layouts  1.02 us (3%)
  between operations  0.66 us (2%)
    pallas_call x1, Pallas kernels, on_device(): pl.pallas_call(functools.partial(exchange_kernel, *sizes), out_shape=(sha...  24.1 us
    pallas_call x1, Pallas kernels, on_device(): pl.pallas_call(functools.partial(apply_kernel, 3 * steps, tile), out_shap...  3.35 us
    unnamed x4, local copies, waits for them, and re-layouts  1.02 us

profile of v3, /device:TPU:0, one launch (start us, length us, event | category | flops | bytes accessed | tf_op | source)
XLA Modules:
  0.0 29.1 jit_solution(15892545936528173001)
XLA Ops:
  0.6 0.0 copy-start
  0.6 24.1 %exchange.1 = (bf16[48,4864]{1,0:T(8,128)(2,1)}, f32[1,1]{1,0:T(1,128)}) custom-call(s32[16]{0:T(128)} %sites_hbm.1, s32[32,128]{1,0:T(8,128)} %bitcast.6, s32[16]{0:T(128)} %accept_hbm.1, f32[256,4096]{1,0:T(8,128)} %bitcast.4), custom_call_target="tpu_custom_call" | custom-call | flops 1000000000 | bytes 67108864 | tf_op jit(solution)/shard_map/exchange/pallas_call | solution.py:271
  24.7 0.0 copy-done
  24.7 0.0 copy-start.1
  24.7 1.0 %copy-done.1 = bf16[48,4864]{1,0:T(8,128)(2,1)S(1)} copy-done((bf16[48,4864]{1,0:T(8,128)(2,1)S(1)}, bf16[48,4864]{1,0:T(8,128)(2,1)}, u32[]{:S(2)}) %copy-start.1) | copy-done | bytes 466968
  25.8 3.3 %apply.1 = (f32[256,4096]{1,0:T(8,128)}, f32[1,1]{1,0:T(1,128)}) custom-call(bf16[48,4864]{1,0:T(8,128)(2,1)S(1)} %copy-done.1, f32[1,1]{1,0:T(1,128)} %get-tuple-element.7.total_ref, f32[256,4096]{1,0:T(8,128)S(1)} %bitcast.5), custom_call_target="tpu_custom_call" | custom-call | flops 100663296 | bytes 8388608 | tf_op jit(solution)/shard_map/apply/pallas_call | solution.py:299
Async XLA Ops:
  0.6 24.1 %copy-start = (f32[1,256,4096]{2,1,0:T(8,128)S(1)}, f32[1,256,4096]{2,1,0:T(8,128)}, u32[]{:S(2)}) copy-start(f32[1,256,4096]{2,1,0:T(8,128)} %param.4) | copy-start | bytes 12582916
  24.7 1.0 %copy-start.1 = (bf16[48,4864]{1,0:T(8,128)(2,1)S(1)}, bf16[48,4864]{1,0:T(8,128)(2,1)}, u32[]{:S(2)}) copy-start(bf16[48,4864]{1,0:T(8,128)(2,1)} %get-tuple-element.6.vst_ref) | copy-start | bytes 1400836
